TPU v7x, 32 devices: a whole 2x2x4 slice. The times are simulated.
32 devices in a mesh: seq: 8 (over z, x), mp: 4 (over y, core).
Axes of the slice: x: 2, y: 2, z: 4, core: 2. Of those that a mesh axis runs over, the one named last changes fastest.
Arguments:
- grad_rows: bfloat16 [4096, 8192], P('seq', 'mp'), may hold values from -6 to 6
- img_start: int32 [64], replicated, may hold values from 0 to 4092, as said below
- img_len: int32 [64], replicated, may hold values from 4 to 64, as said below
- img_owner: int32 [64], replicated, may hold values from 0 to 7, as said below
- pre_act: bfloat16 [4096, 5120], P('seq', 'mp'), may hold values from -6 to 6
- w_out: bfloat16 [5120, 8192], P(None, 'mp'), may hold values from -0.0625 to 0.0625
Outputs:
- pre_grad: bfloat16 [4096, 5120], P('seq', 'mp')
- weight_grad: bfloat16 [5120, 8192], P('seq', 'mp')
Inputs may be any that keep to these rules, and one draw needn't show every extreme that they name: Image i lies inside positions i * 64 to (i + 1) * 64 - 1: img_start[i] - i * 64 + img_len[i] <= 64. `img_len`: A multiple of 4. In every draw some owner has all its images of exactly 64 merged tokens. `img_owner`: the images i with one value of i % 8 all have different owners, and so do the 8 images of one stripe (images i with one value of i // 8).
All inputs are finite; a program needn't handle non-finite values.
Results may differ from a plain program's by a relative error of at most 0.02.
Values may be sent and summed in bfloat16 or wider, within the bound.
A program may use at most 192 MiB of HBM per device.

v0:
```python
import math
import jax
import jax.numpy as jnp
from jax import lax
from jax.sharding import PartitionSpec as P

FRAME = 64


def gelu_parts(values):
    normal_cdf = 0.5 * (1.0 + lax.erf(values * 0.7071067811865476))
    density = jnp.exp(-0.5 * values * values) * 0.3989422804014327
    return (values * normal_cdf, normal_cdf + values * density)


def local(grad_rows, img_start, img_len, img_owner, pre_act, w_out):
    stripe = grad_rows.shape[0]
    quarter = grad_rows.shape[1]
    frames = stripe // FRAME
    owners_total = lax.axis_size("seq")
    here = lax.axis_index("seq")
    within = jnp.arange(FRAME, dtype=jnp.int32)
    first_image = here * frames
    starts = lax.dynamic_slice_in_dim(img_start, first_image, frames)
    lengths = lax.dynamic_slice_in_dim(img_len, first_image, frames)
    my_owners = lax.dynamic_slice_in_dim(img_owner, first_image, frames)
    offsets = starts - here * stripe
    row_ids = jnp.clip(offsets[:, None] + within[None, :], 0, stripe - 1)
    filled = within[None, :] < lengths[:, None]
    blocks = jnp.where(filled[:, :, None], grad_rows[row_ids], jnp.zeros((), jnp.bfloat16))
    owner_ids = jnp.arange(owners_total, dtype=jnp.int32)
    placing = (my_owners[None, :] == owner_ids[:, None]).astype(jnp.bfloat16)
    outgoing = jnp.dot(
        placing, blocks.reshape(frames, FRAME * quarter), preferred_element_type=jnp.float32
    )
    outgoing = outgoing.astype(jnp.bfloat16).reshape(owners_total * FRAME, quarter)
    received = lax.all_to_all(outgoing, "seq", split_axis=0, concat_axis=0, tiled=True)
    choosing = (img_owner.reshape(owners_total, frames) == here).T.astype(jnp.bfloat16)
    routed = jnp.dot(
        choosing,
        received.reshape(owners_total, FRAME * quarter),
        preferred_element_type=jnp.float32,
    )
    routed = routed.astype(jnp.bfloat16).reshape(stripe, quarter)
    hidden_terms = lax.dot_general(
        routed, w_out, (((1,), (1,)), ((), ())), preferred_element_type=jnp.float32
    )
    hidden_grad = lax.psum_scatter(
        hidden_terms.astype(jnp.bfloat16), "mp", scatter_dimension=1, tiled=True
    ).astype(jnp.float32)
    _, derivative = gelu_parts(pre_act.astype(jnp.float32))
    pre_grad = (hidden_grad * derivative).astype(jnp.bfloat16)
    pre_full = lax.all_gather(pre_act, "mp", axis=1, tiled=True)
    activation, _ = gelu_parts(pre_full.astype(jnp.float32))
    activation = activation.astype(jnp.bfloat16)
    factor = 1.0 / math.sqrt(owners_total * stripe)
    kept_rows = activation.shape[1] // owners_total
    act_columns = lax.all_to_all(activation, "seq", split_axis=1, concat_axis=0, tiled=True)
    shard_rows = lax.all_gather(routed, "seq", axis=0, tiled=True)
    owners_here = shard_rows.shape[0] // stripe
    product = (
        jnp.einsum(
            "kar,kaq->krq",
            act_columns.reshape(owners_here, stripe, kept_rows),
            shard_rows.reshape(owners_here, stripe, quarter),
            preferred_element_type=jnp.float32,
        )
        * factor
    )
    product = lax.optimization_barrier(product.astype(jnp.bfloat16))
    weight_grad = jnp.sum(product.astype(jnp.float32), axis=0)
    return (pre_grad, weight_grad.astype(jnp.bfloat16))


def solution(mesh):
    return jax.shard_map(
        local,
        mesh=mesh,
        in_specs=(P("seq", "mp"), P(), P(), P(), P("seq", "mp"), P(None, "mp")),
        out_specs=(P("seq", "mp"), P("seq", "mp")),
        check_vma=False,
    )
```

profile of v0, /device:TPU:0, one launch (start us, length us, event | category | flops | bytes accessed | tf_op | source)
XLA Modules:
  0.0 487.9 jit_solution(11134335510358859104)
XLA Ops:
  7.2 0.0 copy-start
  7.2 0.0 all-gather.3.cloned.1.call-start
  7.2 0.7 all-gather.3.cloned.1.call-update
  7.9 0.7 dynamic-slice_subtract_fusion
  8.7 0.1 compare_select_fusion
  8.7 0.1 reshape.100
  8.8 0.7 dynamic_slice.10
  9.5 0.0 copy-done
  9.6 3.3 gather_fusion
  12.8 0.1 iota_compare_fusion
  12.9 1.8 select_bitcast_fusion
  14.7 0.0 copy-start.5
  14.7 1.2 copy.12
  15.9 0.0 copy-done.5
  15.9 0.1 dynamic_slice.9
  16.0 0.7 convolution_convert_fusion.1
  16.7 2.5 copy.10
  19.1 7.3 %all-to-all-start = ((bf16[8,64,2048]{2,1,0:T(8,128)(2,1)}), bf16[8,64,2048]{2,1,0:T(8,128)(2,1)S(1)}, u32[]{:S(2)}, u32[]{:S(2)}) async-start(bf16[8,64,2048]{2,1,0:T(8,128)(2,1)} %copy.10), calls=%async_computation | async-start | bytes 4194304 | tf_op jit(solution)/shard_map/all_to_all | solution.py:37
  26.4 0.2 reduce-scatter.2.cloned.1.call-start
  26.7 0.1 eq.24
  26.7 47.9 %all-to-all-done = bf16[8,64,2048]{2,1,0:T(8,128)(2,1)S(1)} async-done(((bf16[8,64,2048]{2,1,0:T(8,128)(2,1)}), bf16[8,64,2048]{2,1,0:T(8,128)(2,1)S(1)}, u32[]{:S(2)}, u32[]{:S(2)}) %all-to-all-start) | async-done | bytes 2097184 | tf_op jit(solution)/shard_map/all_to_all | solution.py:37
  74.7 0.0 copy-start.3
  74.7 1.3 copy-done.3
  76.0 2.7 copy.13
  78.7 2.0 convolution_convert_fusion
  80.7 2.5 reshape.96
  83.2 0.0 copy-start.2
  83.2 17.5 %convolution_convert_fusion.2 = bf16[512,5120]{1,0:T(8,128)(2,1)} fusion(bf16[512,2048]{1,0:T(8,128)(2,1)S(1)} %reshape.96, bf16[5120,2048]{1,0:T(8,128)(2,1)} %param.11), kind=kOutput, calls=%fused_computation.10 | convolution fusion | flops 10740039680 | bytes 28311552 | tf_op jit(solution)/shard_map/dot_general | solution.py:45
  100.7 0.0 copy-done.2
  100.7 0.0 reduce-scatter.2.cloned.1.call-update
  100.8 0.0 all-gather.5.cloned.1.call-start
  100.8 0.7 all-gather.5.cloned.1.call-update
  101.5 0.0 all-gather.3.cloned.1.call-done
  101.5 6.6 %fusion.3 = bf16[512,5120]{1,0:T(8,128)(2,1)} fusion(bf16[512,5120]{1,0:T(8,128)(2,1)} %all-gather.3.cloned.1.call-done), kind=kLoop, calls=%fused_computation.9 | loop fusion | flops 15728640 | bytes 10485760 | tf_op jit(solution)/shard_map/convert_element_type | solution.py:55
  108.1 7.7 %copy.11 = bf16[512,5120]{0,1:T(8,128)(2,1)} copy(bf16[512,5120]{1,0:T(8,128)(2,1)} %fusion.3) | data formatting | bytes 10485760 | tf_op jit(solution)/shard_map/convert_element_type | solution.py:55
  115.9 0.0 copy-start.4
  115.9 5.0 %all-to-all-start.1 = ((bf16[512,8,640]{0,2,1:T(8,128)(2,1)}), bf16[512,8,640]{0,2,1:T(8,128)(2,1)}, u32[]{:S(2)}, u32[]{:S(2)}) async-start(bf16[512,8,640]{0,2,1:T(8,128)(2,1)} %bitcast.20), calls=%async_computation.2 | async-start | bytes 10485760 | tf_op jit(solution)/shard_map/all_to_all | solution.py:58
  120.9 30.3 %reduce-scatter.2.cloned.1.call-done = bf16[512,1280]{1,0:T(8,128)(2,1)} async-done(((bf16[512,5120]{1,0:T(8,128)(2,1)}), bf16[512,1280]{1,0:T(8,128)(2,1)}) %reduce-scatter.2.cloned.1.call-update) | async-done | bytes 1310736 | tf_op jit(solution)/shard_map/reduce_scatter | solution.py:48
  151.2 0.0 copy-done.4
  151.2 3.2 fusion.12
  154.4 144.3 %all-to-all-done.1 = bf16[512,8,640]{0,2,1:T(8,128)(2,1)} async-done(((bf16[512,8,640]{0,2,1:T(8,128)(2,1)}), bf16[512,8,640]{0,2,1:T(8,128)(2,1)}, u32[]{:S(2)}, u32[]{:S(2)}) %all-to-all-start.1) | async-done | bytes 5242912 | tf_op jit(solution)/shard_map/all_to_all | solution.py:58
  298.7 148.5 %all-gather.5.cloned.1.call-done = bf16[4096,2048]{1,0:T(8,128)(2,1)} async-done(((bf16[512,2048]{1,0:T(8,128)(2,1)}), bf16[4096,2048]{1,0:T(8,128)(2,1)}) %all-gather.5.cloned.1.call-update) | async-done | bytes 16777232 | tf_op jit(solution)/shard_map/all_gather | solution.py:59
  447.2 20.8 %multiply_convert_fusion = bf16[8,640,2048]{2,1,0:T(8,128)(2,1)} fusion(bf16[8,512,2048]{2,1,0:T(8,128)(2,1)} %bitcast.26, bf16[512,8,640]{0,2,1:T(8,128)(2,1)} %all-to-all-done.1), kind=kOutput, calls=%fused_computation.3 | convolution fusion | flops 10758389760 | bytes 42991616 | tf_op jit(solution)/shard_map/kar,kaq->krq/dot_general | solution.py:62
  468.0 0.0 copy-start.1
  468.0 13.4 %reduce_sum.12 = bf16[640,2048]{1,0:T(8,128)(2,1)} reduce(bf16[8,640,2048]{2,1,0:T(8,128)(2,1)} %multiply_convert_fusion, bf16[]{:T(256)} %constant.4.clone.1), dimensions={0}, to_apply=%region_1.2 | reduce | flops 9175040 | bytes 23592962 | tf_op jit(solution)/shard_map/reduce_sum | solution.py:71
  481.3 0.0 copy-done.1
  (2 shorter events, 0.0 us)
Async XLA Ops:
  7.2 2.4 copy-start
  7.2 94.3 %all-gather.3.cloned.1.call-start = ((), (), s32[]{:S(2)}) async-start(), calls=%async_computation.4 | async-start | bytes 6553600 | tf_op jit(solution)/shard_map/all_gather | solution.py:53
  14.7 1.2 copy-start.5
  19.1 55.5 %all-to-all-start = ((bf16[8,64,2048]{2,1,0:T(8,128)(2,1)}), bf16[8,64,2048]{2,1,0:T(8,128)(2,1)S(1)}, u32[]{:S(2)}, u32[]{:S(2)}) async-start(bf16[8,64,2048]{2,1,0:T(8,128)(2,1)} %copy.10), calls=%async_computation | async-start | bytes 4194304 | tf_op jit(solution)/shard_map/all_to_all | solution.py:37
  26.4 124.8 %reduce-scatter.2.cloned.1.call-start = ((), (), s32[]{:S(2)}) async-start(), calls=%async_computation.3 | async-start | bytes 6553600 | tf_op jit(solution)/shard_map/reduce_scatter | solution.py:48
  74.7 1.3 copy-start.3
  83.2 17.5 %copy-start.2 = (bf16[512,2048]{1,0:T(8,128)(2,1)}, bf16[512,2048]{1,0:T(8,128)(2,1)S(1)}, u32[]{:S(2)}) copy-start(bf16[512,2048]{1,0:T(8,128)(2,1)S(1)} %reshape.96) | copy-start | bytes 6291460
  100.8 346.4 %all-gather.5.cloned.1.call-start = ((), (), s32[]{:S(2)}) async-start(), calls=%async_computation.5 | async-start | bytes 18874368 | tf_op jit(solution)/shard_map/all_gather | solution.py:59
  115.9 35.3 %copy-start.4 = (bf16[512,1280]{1,0:T(8,128)(2,1)S(1)}, bf16[512,1280]{1,0:T(8,128)(2,1)}, u32[]{:S(2)}) copy-start(bf16[512,1280]{1,0:T(8,128)(2,1)} %param.10) | copy-start | bytes 3932164
  115.9 182.8 %all-to-all-start.1 = ((bf16[512,8,640]{0,2,1:T(8,128)(2,1)}), bf16[512,8,640]{0,2,1:T(8,128)(2,1)}, u32[]{:S(2)}, u32[]{:S(2)}) async-start(bf16[512,8,640]{0,2,1:T(8,128)(2,1)} %bitcast.20), calls=%async_computation.2 | async-start | bytes 10485760 | tf_op jit(solution)/shard_map/all_to_all | solution.py:58
  468.0 13.4 %copy-start.1 = (bf16[512,2048]{1,0:T(8,128)(2,1)S(1)}, bf16[512,2048]{1,0:T(8,128)(2,1)}, u32[]{:S(2)}) copy-start(bf16[512,2048]{1,0:T(8,128)(2,1)} %param.6) | copy-start | bytes 6291460
Sparse Core Ops, SparseCore 0:
  9.5 43.1 all-gather.2
  100.9 50.2 reduce-scatter.1
  153.9 293.2 all-gather.4
where the time goes:
time: 489 us; the launch traced here: 488 us
  waiting for transfers between devices  372 us (76%)
  matrix products  40.9 us (8%)
  other arithmetic  25.8 us (5%)
  local copies, waits for them, and re-layouts  22.3 us (5%)
  between operations  13.8 us (3%)
  starting transfers between devices  12.6 us (3%)
    all_gather x1, waiting for transfers between devices, local(): shard_rows = lax.all_gather(routed, 'seq', axis=0, tiled=True)  148 us
    all_to_all x1, waiting for transfers between devices, local(): lax.all_to_all(activation, 'seq', split_axis=1, concat_axis=0, tiled=True)  144 us
    all_to_all x1, waiting for transfers between devices, local(): lax.all_to_all(outgoing, 'seq', split_axis=0, concat_axis=0, tiled=True)  47.9 us
    reduce_scatter x1, waiting for transfers between devices, local(): lax.psum_scatter(hidden_terms.astype(jnp.bfloat16), 'mp', scatter_dimensi...  30.3 us
    dot_general x1, matrix products, local(): jnp.einsum('kar,kaq->krq', act_columns.reshape(owners_here, stripe, kept_...  20.8 us
    dot_general x1, matrix products, local(): lax.dot_general(routed, w_out, (((1,), (1,)), ((), ())), preferred_elemen...  17.5 us
    reduce_sum x1, other arithmetic, local(): weight_grad = jnp.sum(product.astype(jnp.float32), axis=0)  13.4 us
  transfers between devices with their start and end apart: 5, of which 4 were waited for; matrix products, arithmetic and copies ran while one was open for 11% of the time, Pallas kernels for 0%

commit v1 on v0

--- a/solution.py
+++ b/solution.py
@@ -56,7 +56,12 @@
     factor = 1.0 / math.sqrt(owners_total * stripe)
     kept_rows = activation.shape[1] // owners_total
     act_columns = lax.all_to_all(activation, "seq", split_axis=1, concat_axis=0, tiled=True)
-    shard_rows = lax.all_gather(routed, "seq", axis=0, tiled=True)
+    ring = [routed]
+    for hop in range(7):
+        ring.append(lax.ppermute(ring[-1], "seq", [(dev, (dev + 1) % 8) for dev in range(8)]))
+    shard_rows = jnp.roll(
+        jnp.concatenate(ring[::-1], axis=0), (lax.axis_index("seq") + 1) * ring[0].shape[0], axis=0
+    )
     owners_here = shard_rows.shape[0] // stripe
     product = (
         jnp.einsum(

time: 489 us -> 584 us (1.19)
  the two profiles are of different devices: /device:TPU:0 before, /device:TPU:16 now
where the time goes in v1:
time: 584 us; the launch traced here: 583 us
  waiting for transfers between devices  415 us (71%)
  local copies, waits for them, and re-layouts  50.9 us (9%)
  matrix products  40.2 us (7%)
  starting transfers between devices  36.6 us (6%)
  other arithmetic  25.7 us (4%)
  between operations  14.2 us (2%)
    ppermute x7, waiting for transfers between devices, local(): lax.ppermute(ring[-1], 'seq', [(dev, (dev + 1) % 8) for dev in range(8)])  370 us
    all_to_all x1, waiting for transfers between devices, local(): lax.all_to_all(outgoing, 'seq', split_axis=0, concat_axis=0, tiled=True)  44.1 us
    unnamed x35, local copies, waits for them, and re-layouts  26.8 us
    dot_general x1, matrix products, local(): jnp.einsum('kar,kaq->krq', act_columns.reshape(owners_here, stripe, kept_...  20.7 us
    ppermute x7, starting transfers between devices, local(): lax.ppermute(ring[-1], 'seq', [(dev, (dev + 1) % 8) for dev in range(8)])  20 us
    dot_general x1, matrix products, local(): lax.dot_general(routed, w_out, (((1,), (1,)), ((), ())), preferred_elemen...  16.8 us
    reduce_sum x1, other arithmetic, local(): weight_grad = jnp.sum(product.astype(jnp.float32), axis=0)  13.4 us
  transfers between devices with their start and end apart: 11, of which 8 were waited for; matrix products, arithmetic and copies ran while one was open for 12% of the time, Pallas kernels for 0%

profile of v1, /device:TPU:16, one launch (start us, length us, event | category | flops | bytes accessed | tf_op | source)
XLA Modules:
  0.0 582.6 jit_solution(10587824623787970456)
XLA Ops:
  7.2 0.9 dynamic-slice_subtract_fusion
  8.2 0.7 dynamic_slice.14
  9.0 3.3 gather_fusion
  12.3 1.8 select_bitcast_fusion
  14.1 1.2 copy.12
  15.4 0.7 convolution_convert_fusion.1
  16.1 2.5 copy.10
  18.6 6.1 %all-to-all-start = ((bf16[8,64,2048]{2,1,0:T(8,128)(2,1)}), bf16[8,64,2048]{2,1,0:T(8,128)(2,1)S(1)}, u32[]{:S(2)}, u32[]{:S(2)}) async-start(bf16[8,64,2048]{2,1,0:T(8,128)(2,1)} %copy.10), calls=%async_computation | async-start | bytes 4194304 | tf_op jit(solution)/shard_map/all_to_all | solution.py:37
  24.7 0.7 all-gather.2.cloned.1.call-update
  25.6 44.1 %all-to-all-done = bf16[8,64,2048]{2,1,0:T(8,128)(2,1)S(1)} async-done(((bf16[8,64,2048]{2,1,0:T(8,128)(2,1)}), bf16[8,64,2048]{2,1,0:T(8,128)(2,1)S(1)}, u32[]{:S(2)}, u32[]{:S(2)}) %all-to-all-start) | async-done | bytes 2097184 | tf_op jit(solution)/shard_map/all_to_all | solution.py:37
  69.7 1.3 copy-done.6
  71.0 2.7 copy.13
  73.7 2.0 convolution_convert_fusion
  75.7 2.5 reshape.96
  78.2 1.5 collective-permute-start
  79.7 45.9 %collective-permute-done = bf16[512,2048]{1,0:T(8,128)(2,1)} collective-permute-done((bf16[512,2048]{1,0:T(8,128)(2,1)S(1)}, bf16[512,2048]{1,0:T(8,128)(2,1)}, u32[]{:S(2)}, u32[]{:S(2)}) %collective-permute-start) | collective-permute-done | bytes 2097184 | tf_op jit(solution)/shard_map/ppermute | solution.py:61
  125.7 2.3 collective-permute-start.1
  128.0 16.8 %convolution_convert_fusion.2 = bf16[512,5120]{1,0:T(8,128)(2,1)} fusion(bf16[512,2048]{1,0:T(8,128)(2,1)S(1)} %reshape.96, bf16[5120,2048]{1,0:T(8,128)(2,1)} %param.11), kind=kOutput, calls=%fused_computation.10 | convolution fusion | flops 10740039680 | bytes 28311552 | tf_op jit(solution)/shard_map/dot_general | solution.py:45
  144.8 27.9 %collective-permute-done.1 = bf16[512,2048]{1,0:T(8,128)(2,1)} collective-permute-done((bf16[512,2048]{1,0:T(8,128)(2,1)}, bf16[512,2048]{1,0:T(8,128)(2,1)}, u32[]{:S(2)}, u32[]{:S(2)}) %collective-permute-start.1) | collective-permute-done | bytes 2097184 | tf_op jit(solution)/shard_map/ppermute | solution.py:61
  172.7 3.3 collective-permute-start.2
  176.0 43.7 %collective-permute-done.2 = bf16[512,2048]{1,0:T(8,128)(2,1)S(1)} collective-permute-done((bf16[512,2048]{1,0:T(8,128)(2,1)}, bf16[512,2048]{1,0:T(8,128)(2,1)S(1)}, u32[]{:S(2)}, u32[]{:S(2)}) %collective-permute-start.2) | collective-permute-done | bytes 2097184 | tf_op jit(solution)/shard_map/ppermute | solution.py:61
  219.7 1.4 copy-done.2
  221.1 3.4 collective-permute-start.3
  224.5 42.5 %collective-permute-done.3 = bf16[512,2048]{1,0:T(8,128)(2,1)S(1)} collective-permute-done((bf16[512,2048]{1,0:T(8,128)(2,1)S(1)}, bf16[512,2048]{1,0:T(8,128)(2,1)S(1)}, u32[]{:S(2)}, u32[]{:S(2)}) %collective-permute-start.3) | collective-permute-done | bytes 2097184 | tf_op jit(solution)/shard_map/ppermute | solution.py:61
  267.0 1.3 copy-done.4
  268.3 3.3 collective-permute-start.4
  271.6 42.3 %collective-permute-done.4 = bf16[512,2048]{1,0:T(8,128)(2,1)} collective-permute-done((bf16[512,2048]{1,0:T(8,128)(2,1)S(1)}, bf16[512,2048]{1,0:T(8,128)(2,1)}, u32[]{:S(2)}, u32[]{:S(2)}) %collective-permute-start.4) | collective-permute-done | bytes 2097184 | tf_op jit(solution)/shard_map/ppermute | solution.py:61
  313.9 3.2 collective-permute-start.5
  317.1 6.3 %fusion.3 = bf16[512,5120]{1,0:T(8,128)(2,1)} fusion(bf16[512,5120]{1,0:T(8,128)(2,1)} %all-gather.2.cloned.1.call-done), kind=kLoop, calls=%fused_computation.9 | loop fusion | flops 15728640 | bytes 10485760 | tf_op jit(solution)/shard_map/convert_element_type | solution.py:55
  323.4 7.9 %copy.11 = bf16[512,5120]{0,1:T(8,128)(2,1)} copy(bf16[512,5120]{1,0:T(8,128)(2,1)} %fusion.3) | data formatting | bytes 10485760 | tf_op jit(solution)/shard_map/convert_element_type | solution.py:55
  331.3 10.4 %all-to-all-start.1 = ((bf16[512,8,640]{0,2,1:T(8,128)(2,1)}), bf16[512,8,640]{0,2,1:T(8,128)(2,1)}, u32[]{:S(2)}, u32[]{:S(2)}) async-start(bf16[512,8,640]{0,2,1:T(8,128)(2,1)} %bitcast.20), calls=%async_computation.2 | async-start | bytes 10485760 | tf_op jit(solution)/shard_map/all_to_all | solution.py:58
  341.7 55.5 %collective-permute-done.5 = bf16[512,2048]{1,0:T(8,128)(2,1)} collective-permute-done((bf16[512,2048]{1,0:T(8,128)(2,1)}, bf16[512,2048]{1,0:T(8,128)(2,1)}, u32[]{:S(2)}, u32[]{:S(2)}) %collective-permute-start.5) | collective-permute-done | bytes 2097184 | tf_op jit(solution)/shard_map/ppermute | solution.py:61
  397.2 3.0 collective-permute-start.6
  400.2 3.2 fusion.12
  403.4 112.4 %collective-permute-done.6 = bf16[512,2048]{1,0:T(8,128)(2,1)} collective-permute-done((bf16[512,2048]{1,0:T(8,128)(2,1)}, bf16[512,2048]{1,0:T(8,128)(2,1)}, u32[]{:S(2)}, u32[]{:S(2)}) %collective-permute-start.6) | collective-permute-done | bytes 2097184 | tf_op jit(solution)/shard_map/ppermute | solution.py:61
  515.8 1.7 constant_dynamic-update-slice_fusion.15
  517.6 1.9 constant_dynamic-update-slice_fusion.14
  519.5 1.9 constant_dynamic-update-slice_fusion.13
  522.0 1.7 constant_dynamic-update-slice_fusion.10
  523.7 1.7 constant_dynamic-update-slice_fusion.9
  525.6 1.7 constant_dynamic-update-slice_fusion.7
  527.3 1.7 constant_dynamic-update-slice_fusion.6
  529.1 1.7 constant_dynamic-update-slice_fusion.5
  531.3 1.7 constant_dynamic-update-slice_fusion.2
  533.0 1.7 constant_dynamic-update-slice_fusion.1
  534.9 6.7 %constant_dynamic-slice_fusion = bf16[4096,2048]{1,0:T(8,128)(2,1)} fusion(bf16[8192,2048]{1,0:T(8,128)(2,1)S(1)} %constant_dynamic-update-slice_fusion, s32[]{:T(128)S(6)} %select_n.41), kind=kLoop, calls=%fused_computation.47 | loop fusion | bytes 33554436 | tf_op jit(solution)/shard_map/jit(_roll_dynamic)/dynamic_slice | solution.py:62
  541.6 20.7 %multiply_convert_fusion = bf16[8,640,2048]{2,1,0:T(8,128)(2,1)} fusion(bf16[8,512,2048]{2,1,0:T(8,128)(2,1)} %bitcast.21, bf16[512,8,640]{0,2,1:T(8,128)(2,1)} %all-to-all-done.1), kind=kOutput, calls=%fused_computation.3 | convolution fusion | flops 10758389760 | bytes 42991616 | tf_op jit(solution)/shard_map/kar,kaq->krq/dot_general | solution.py:67
  562.4 13.4 %reduce_sum.12 = bf16[640,2048]{1,0:T(8,128)(2,1)} reduce(bf16[8,640,2048]{2,1,0:T(8,128)(2,1)} %multiply_convert_fusion, bf16[]{:T(256)} %constant.25.clone.1), dimensions={0}, to_apply=%region_1.2 | reduce | flops 9175040 | bytes 23592962 | tf_op jit(solution)/shard_map/reduce_sum | solution.py:76
  (34 shorter events, 1.9 us)
Async XLA Ops:
  7.2 1.9 copy-start
  12.3 3.0 copy-start.8
  18.6 51.1 %all-to-all-start = ((bf16[8,64,2048]{2,1,0:T(8,128)(2,1)}), bf16[8,64,2048]{2,1,0:T(8,128)(2,1)S(1)}, u32[]{:S(2)}, u32[]{:S(2)}) async-start(bf16[8,64,2048]{2,1,0:T(8,128)(2,1)} %copy.10), calls=%async_computation | async-start | bytes 4194304 | tf_op jit(solution)/shard_map/all_to_all | solution.py:37
  24.7 292.4 %all-gather.2.cloned.1.call-start = ((), (), s32[]{:S(2)}) async-start(), calls=%async_computation.4 | async-start | bytes 6553600 | tf_op jit(solution)/shard_map/all_gather | solution.py:53
  25.4 374.8 %reduce-scatter.2.cloned.1.call-start = ((), (), s32[]{:S(2)}) async-start(), calls=%async_computation.3 | async-start | bytes 6553600 | tf_op jit(solution)/shard_map/reduce_scatter | solution.py:48
  69.7 1.3 copy-start.6
  78.2 47.4 %collective-permute-start = (bf16[512,2048]{1,0:T(8,128)(2,1)S(1)}, bf16[512,2048]{1,0:T(8,128)(2,1)}, u32[]{:S(2)}, u32[]{:S(2)}) collective-permute-start(bf16[512,2048]{1,0:T(8,128)(2,1)S(1)} %reshape.96), channel_id=1, source_target_pairs={{0,4},{4,8},{8,12},{12,16},{16,20},{20,24},{24,28},{28,0},{1,5},{5... | collective-permute-start | bytes 6291464 | tf_op jit(solution)/shard_map/ppermute | solution.py:61
  125.7 47.0 %collective-permute-start.1 = (bf16[512,2048]{1,0:T(8,128)(2,1)}, bf16[512,2048]{1,0:T(8,128)(2,1)}, u32[]{:S(2)}, u32[]{:S(2)}) collective-permute-start(bf16[512,2048]{1,0:T(8,128)(2,1)} %collective-permute-done), channel_id=1, source_target_pairs={{0,4},{4,8},{8,12},{12,16},{16,20},{20,24},{24,28},{28,0},{1,5},{5... | collective-permute-start | bytes 6291464 | tf_op jit(solution)/shard_map/ppermute | solution.py:61
  172.7 47.0 %collective-permute-start.2 = (bf16[512,2048]{1,0:T(8,128)(2,1)}, bf16[512,2048]{1,0:T(8,128)(2,1)S(1)}, u32[]{:S(2)}, u32[]{:S(2)}) collective-permute-start(bf16[512,2048]{1,0:T(8,128)(2,1)} %collective-permute-done.1), channel_id=1, source_target_pairs={{0,4},{4,8},{8,12},{12,16},{16,20},{20,24},{24,28},{28,0},{1,5},{5... | collective-permute-start | bytes 6291464 | tf_op jit(solution)/shard_map/ppermute | solution.py:61
  219.7 1.4 copy-start.2
  221.1 45.9 %collective-permute-start.3 = (bf16[512,2048]{1,0:T(8,128)(2,1)S(1)}, bf16[512,2048]{1,0:T(8,128)(2,1)S(1)}, u32[]{:S(2)}, u32[]{:S(2)}) collective-permute-start(bf16[512,2048]{1,0:T(8,128)(2,1)S(1)} %collective-permute-done.2), channel_id=1, source_target_pairs={{0,4},{4,8},{8,12},{12,16},{16,20},{20,24},{24,28},{28,0},{1,5},{5... | collective-permute-start | bytes 6291464 | tf_op jit(solution)/shard_map/ppermute | solution.py:61
  267.0 1.3 copy-start.4
  268.3 45.6 %collective-permute-start.4 = (bf16[512,2048]{1,0:T(8,128)(2,1)S(1)}, bf16[512,2048]{1,0:T(8,128)(2,1)}, u32[]{:S(2)}, u32[]{:S(2)}) collective-permute-start(bf16[512,2048]{1,0:T(8,128)(2,1)S(1)} %collective-permute-done.3), channel_id=1, source_target_pairs={{0,4},{4,8},{8,12},{12,16},{16,20},{20,24},{24,28},{28,0},{1,5},{5... | collective-permute-start | bytes 6291464 | tf_op jit(solution)/shard_map/ppermute | solution.py:61
  313.9 83.3 %collective-permute-start.5 = (bf16[512,2048]{1,0:T(8,128)(2,1)}, bf16[512,2048]{1,0:T(8,128)(2,1)}, u32[]{:S(2)}, u32[]{:S(2)}) collective-permute-start(bf16[512,2048]{1,0:T(8,128)(2,1)} %collective-permute-done.4), channel_id=1, source_target_pairs={{0,4},{4,8},{8,12},{12,16},{16,20},{20,24},{24,28},{28,0},{1,5},{5... | collective-permute-start | bytes 6291464 | tf_op jit(solution)/shard_map/ppermute | solution.py:61
  331.3 68.9 %copy-start.7 = (bf16[512,1280]{1,0:T(8,128)(2,1)S(1)}, bf16[512,1280]{1,0:T(8,128)(2,1)}, u32[]{:S(2)}) copy-start(bf16[512,1280]{1,0:T(8,128)(2,1)} %param.10) | copy-start | bytes 3932164
  331.3 210.3 %all-to-all-start.1 = ((bf16[512,8,640]{0,2,1:T(8,128)(2,1)}), bf16[512,8,640]{0,2,1:T(8,128)(2,1)}, u32[]{:S(2)}, u32[]{:S(2)}) async-start(bf16[512,8,640]{0,2,1:T(8,128)(2,1)} %bitcast.20), calls=%async_computation.2 | async-start | bytes 10485760 | tf_op jit(solution)/shard_map/all_to_all | solution.py:58
  397.2 118.6 %collective-permute-start.6 = (bf16[512,2048]{1,0:T(8,128)(2,1)}, bf16[512,2048]{1,0:T(8,128)(2,1)}, u32[]{:S(2)}, u32[]{:S(2)}) collective-permute-start(bf16[512,2048]{1,0:T(8,128)(2,1)} %collective-permute-done.5), channel_id=1, source_target_pairs={{0,4},{4,8},{8,12},{12,16},{16,20},{20,24},{24,28},{28,0},{1,5},{5... | collective-permute-start | bytes 6291464 | tf_op jit(solution)/shard_map/ppermute | solution.py:61
  517.5 3.8 copy-start.5
  519.4 2.3 copy-start.3
  562.4 13.4 %copy-start.1 = (bf16[512,2048]{1,0:T(8,128)(2,1)S(1)}, bf16[512,2048]{1,0:T(8,128)(2,1)}, u32[]{:S(2)}) copy-start(bf16[512,2048]{1,0:T(8,128)(2,1)} %param.6) | copy-start | bytes 6291460
Sparse Core Ops, SparseCore 0:
  27.0 41.3 all-gather.1
  144.9 54.7 reduce-scatter.1
